TPU v7x, 32 devices: a whole 2x2x4 slice. The times are simulated.
32 devices in a mesh: member: 2 (over x), gx: 16 (over z, y, core).
Axes of the slice: x: 2, y: 2, z: 4, core: 2. Of those that a mesh axis runs over, the one named last changes fastest.
Arguments:
- spectrum: float32 [36, 32, 256, 128], P(None, None, ('member', 'gx')), parts along dimension 2, may hold values from 0 to 1
- wind: float32 [2, 256, 128], P(None, ('member', 'gx')), parts along dimension 1, may hold values from -32 to 32
- land_sea: int32 [128, 128], P('gx'), may hold values 0 or 1
- band_rows: int32 [128], replicated, may hold values from 0 to 127, each once
Outputs:
- spectrum_next: float32 [36, 32, 256, 128], P(None, None, ('member', 'gx')), parts along dimension 2
- ocean_fields: float32 [4, 128, 256], P(None, 'gx', 'member'), parts along dimension 2
There are 2 independent parts, one for each index of `member`. A program takes and returns all parts, laid end to end along the dimension named above; an argument that names none is the same for every part. Nothing has to cross between parts.
Inputs may be any that keep to these rules, and one draw needn't show every extreme that they name: band_rows names each of the 128 latitude rows exactly once.
All inputs are finite; a program needn't handle non-finite values. No bound on the sum of `land_sea` on one device may be relied on, other than what follows from the above.
Results may differ from a plain program's by a relative error of at most 0.00015.
Values sent between devices are 32-bit elements; how exact they have to be, the bound alone decides.
A program may use at most 128 MiB of HBM per device.

v0:
```python
import math
import jax
import jax.numpy as jnp
from jax import lax
from jax.sharding import PartitionSpec as P

STEPS = 3


def passed_along(value, axis, steps):
    count = lax.axis_size(axis)
    pairs = [(source, (source + steps) % count) for source in range(count)]
    return lax.ppermute(value, axis, pairs)


def wave_tables(directions, frequencies):
    angles = (jnp.arange(directions, dtype=jnp.float32) + 0.5) * (2.0 * math.pi / directions)
    levels = jnp.arange(frequencies, dtype=jnp.float32)
    shrink = jnp.power(jnp.float32(1.1), -levels)
    frequency = 0.0418 / shrink
    inverse_speed = 2.0 * math.pi * frequency / 9.81
    weight = (levels + 1.0) / frequencies
    cosine_dir = jnp.cos(angles)[:, None]
    sine_dir = jnp.sin(angles)[:, None]
    courant_x = 0.45 * shrink[None, :] * cosine_dir
    courant_y = 0.45 * shrink[None, :] * sine_dir
    factor = 3.0 / math.sqrt(directions * frequencies)
    project = jnp.stack(
        [factor * weight[None, :] * cosine_dir, factor * weight[None, :] * sine_dir]
    )
    return (courant_x, courant_y, cosine_dir, sine_dir, inverse_speed, weight * weight, project)


def upwind(center, west_cell, east_cell, courant_x, courant_y):
    along_x = courant_x[:, :, None, None]
    along_y = courant_y[:, :, None, None]
    border = jnp.zeros_like(center[..., :1])
    south_cell = jnp.concatenate([border, center[..., :-1]], axis=3)
    north_cell = jnp.concatenate([center[..., 1:], border], axis=3)
    return (
        center
        - jnp.maximum(along_x, 0.0) * (center - west_cell)
        + jnp.maximum(-along_x, 0.0) * (east_cell - center)
        - jnp.maximum(along_y, 0.0) * (center - south_cell)
        + jnp.maximum(-along_y, 0.0) * (north_cell - center)
    )


def sources(advected, wind_east, wind_north, sea_mask, tables):
    cosine_dir, sine_dir, inverse_speed, weight_two = (tables[2], tables[3], tables[4], tables[5])
    advected = advected * sea_mask
    energy = jnp.mean(advected, axis=(0, 1))
    wind_ratio = (
        wind_east * cosine_dir[:, :, None, None] + wind_north * sine_dir[:, :, None, None]
    ) * inverse_speed[None, :, None, None]
    growth = 0.05 * jnp.clip(wind_ratio - 1.0, 0.0, 4.0)
    damping = 0.3 * weight_two[None, :, None, None] * (energy / (0.5 + energy))
    return (advected * (1.0 + growth) / (1.0 + damping), growth * advected)


def coupling_fields(input_flux, current, project):
    stress = jnp.einsum("cij,ijxy->cxy", project, input_flux, precision=lax.Precision.HIGHEST)
    stokes = jnp.einsum("cij,ijxy->cxy", project, current, precision=lax.Precision.HIGHEST)
    return jnp.concatenate([stress, stokes], axis=0)


def per_device(spectrum, wind, land_sea, band_rows):
    tables = wave_tables(spectrum.shape[0], spectrum.shape[1])
    sea_mask = land_sea.astype(jnp.float32)
    current = spectrum
    quarter = spectrum.shape[0] // 4
    east_x = jnp.concatenate([tables[0][:quarter], tables[0][3 * quarter :]], axis=0)
    east_y = jnp.concatenate([tables[1][:quarter], tables[1][3 * quarter :]], axis=0)
    west_x = tables[0][quarter : 3 * quarter]
    west_y = tables[1][quarter : 3 * quarter]
    for step_index in range(STEPS):
        eastward = jnp.concatenate([current[:quarter], current[3 * quarter :]], axis=0)
        westward = current[quarter : 3 * quarter]
        from_west = passed_along(eastward[:, :, -1:], "gx", 1)
        from_east = passed_along(westward[:, :, :1], "gx", -1)
        west_cells = jnp.concatenate([from_west, eastward[:, :, :-1]], axis=2)
        east_cells = jnp.concatenate([westward[:, :, 1:], from_east], axis=2)
        moved_east = upwind(eastward, west_cells, eastward, east_x, east_y)
        moved_west = upwind(westward, westward, east_cells, west_x, west_y)
        advected = jnp.concatenate([moved_east[:quarter], moved_west, moved_east[quarter:]], axis=0)
        current, input_flux = sources(advected, wind[0], wind[1], sea_mask, tables)
    fields = coupling_fields(input_flux, current, tables[6])
    local_rows = jnp.transpose(fields[:, :, band_rows], (0, 2, 1))
    gathered = lax.all_gather(local_rows, "gx", axis=2, tiled=True)
    band_count = local_rows.shape[1] // lax.axis_size("gx")
    ocean_fields = lax.dynamic_slice_in_dim(
        gathered, lax.axis_index("gx") * band_count, band_count, 1
    )
    return (current, ocean_fields)


def solution(mesh):
    placed = (
        P(None, None, ("member", "gx"), None),
        P(None, ("member", "gx"), None),
        P("gx", None),
        P(),
    )
    return jax.shard_map(
        per_device,
        mesh=mesh,
        in_specs=placed,
        out_specs=(P(None, None, ("member", "gx"), None), P(None, "gx", "member")),
        check_vma=False,
    )
```

profile of v0, /device:TPU:0, one launch (start us, length us, event | category | flops | bytes accessed | tf_op | source)
XLA Modules:
  0.0 96.4 jit_solution(8376153678232764763)
XLA Ops:
  0.6 1.8 %fusion.60 = (f32[9,32,8,128]{3,2,1,0:T(8,128)S(1)}, f32[9,32,8,128]{3,2,1,0:T(8,128)S(1)}) fusion(f32[36,32,8,128]{3,2,1,0:T(8,128)} %param.4), kind=kLoop, calls=%fused_computation.121 | loop fusion | bytes 4718592 | tf_op jit(solution)/shard_map/slice | solution.py:77
  2.6 0.2 copy_dynamic-update-slice_fusion
  2.9 0.7 slice.228
  3.6 0.5 collective-permute-start
  4.1 0.8 copy-done
  5.1 5.5 %collective-permute-start.1 = (f32[18,32,1,128]{3,1,2,0:T(8,128)S(1)}, f32[18,32,1,128]{3,1,2,0:T(8,128)S(1)}, u32[]{:S(2)}, u32[]{:S(2)}) collective-permute-start(f32[18,32,1,128]{3,1,2,0:T(8,128)S(1)} %bitcast.18), channel_id=1, source_target_pairs={{0,15},{1,0},{2,1},{3,2},{4,3},{5,4},{6,5},{7,6},{8,7},{9,8},{10,9... | collective-permute-start | bytes 884744 | tf_op jit(solution)/shard_map/ppermute | solution.py:13
  10.6 3.1 %fusion.64 = (f32[18,32,8,127]{3,1,2,0:T(8,128)}, f32[18,32,8,127]{3,1,2,0:T(8,128)}) fusion(f32[18,32,8,128]{3,1,2,0:T(8,128)S(1)} %copy_dynamic-update-slice_fusion), kind=kLoop, calls=%fused_computation.125 | loop fusion | bytes 9363456 | tf_op jit(solution)/shard_map/slice | solution.py:38
  13.7 1.6 %slice.229 = f32[18,32,7,128]{3,1,2,0:T(8,128)} slice(f32[18,32,8,128]{3,1,2,0:T(8,128)S(1)} %copy_dynamic-update-slice_fusion), slice={[0:18], [0:32], [0:7], [0:128]} | slice | bytes 4128768 | tf_op jit(solution)/shard_map/slice | solution.py:81
  15.5 0.8 fusion.59
  16.3 0.2 slice.190
  16.6 1.8 %copy.58 = f32[18,32,8,127]{3,1,2,0:T(8,128)} copy(f32[18,32,8,127]{3,2,1,0:T(8,128)S(1)} %get-tuple-element.20) | data formatting | bytes 4681728
  18.5 1.9 %copy.59 = f32[18,32,8,127]{3,1,2,0:T(8,128)} copy(f32[18,32,8,127]{3,2,1,0:T(8,128)S(1)} %get-tuple-element.21) | data formatting | bytes 4681728
  20.3 1.7 %copy.56 = f32[18,32,7,128]{3,1,2,0:T(8,128)} copy(f32[18,32,7,128]{3,2,1,0:T(8,128)S(1)} %slice.190) | data formatting | bytes 4128768
  22.4 4.0 %fusion.16 = f32[18,32,8,128]{3,1,2,0:T(8,128)S(1)} fusion(f32[18,32,8,128]{3,1,2,0:T(8,128)S(1)} %copy_dynamic-update-slice_fusion, f32[18,32,7,128]{3,1,2,0:T(8,128)} %slice.229, f32[18,32,1,128]{3,1,2,0:T(8,128)S(1)} %collective-permute-done, f32[18,32,8,127]{3,1,2,0:T(8,128)} %get-tuple-element.35, f32[18,32,8,127]{3,1,2,0:T(8,128)} %get-tuple-element.34, ...), kind=kLoop, calls=%fused_computation.43 | loop fusion | flops 7667712 | bytes 11768832 | tf_op jit(solution)/shard_map/add | solution.py:41
  26.4 0.3 fusion.63
  26.7 1.4 %slice-done = f32[18,32,8,128]{3,2,1,0:T(8,128)S(1)} async-done(((f32[36,32,8,128]{3,2,1,0:T(8,128)}), f32[18,32,8,128]{3,2,1,0:T(8,128)S(1)}, s32[]{:S(2)}) %slice-start) | async-done | bytes 2359320 | tf_op jit(solution)/shard_map/slice | solution.py:78
  28.1 0.7 copy-done.1
  28.8 1.7 %fusion.20 = f32[18,32,8,128]{3,1,2,0:T(8,128)S(1)} fusion(f32[18,32,1,128]{3,1,2,0:T(8,128)S(1)} %collective-permute-done.1, f32[18,32,7,128]{3,1,2,0:T(8,128)S(1)} %copy-done.3, f32[18,32,8,127]{3,1,2,0:T(8,128)S(1)} %copy-done.2, f32[18,32,8,127]{3,1,2,0:T(8,128)S(1)} %copy-done.1, f32[18,32,8,128]{3,2,1,0:T(8,128)S(1)} %slice-done, ...), kind=kLoop, calls=%fused_computation.48 | loop fusion | flops 7667712 | bytes 11768832 | tf_op jit(solution)/shard_map/add | solution.py:41
  30.6 0.6 fusion.7
  31.2 1.4 %multiply_divide_fusion.2 = f32[36,32,8,128]{3,1,2,0:T(8,128)S(1)} fusion(f32[9,32,8,128]{3,1,2,0:T(8,128)S(1)} %get-tuple-element.33, f32[18,32,8,128]{3,1,2,0:T(8,128)S(1)} %fusion.20, f32[9,32,8,128]{3,1,2,0:T(8,128)S(1)} %get-tuple-element.32, f32[32,8,128]{2,0,1:T(8,128)S(1)} %multiply_add_fusion.3, f32[32]{0:T(128)S(1)} %power_multiply_fusion, ...), kind=kLoop, calls=%fused_computation.10 | loop fusion | flops 11796480 | bytes 9719936 | tf_op jit(solution)/shard_map/div | solution.py:58
  32.6 0.9 fusion.57
  33.5 0.3 fusion.58
  33.9 0.2 fusion.40
  34.2 0.2 slice.250
  34.4 4.7 %collective-permute-start.3 = (f32[18,32,1,128]{3,1,2,0:T(8,128)S(1)}, f32[18,32,1,128]{3,1,2,0:T(8,128)S(1)}, u32[]{:S(2)}, u32[]{:S(2)}) collective-permute-start(f32[18,32,1,128]{3,1,2,0:T(8,128)S(1)} %slice.251), channel_id=1, source_target_pairs={{0,15},{1,0},{2,1},{3,2},{4,3},{5,4},{6,5},{7,6},{8,7},{9,8},{10,9... | collective-permute-start | bytes 884744 | tf_op jit(solution)/shard_map/ppermute | solution.py:13
  39.1 0.9 fusion.10
  39.9 2.8 %collective-permute-done.2 = f32[18,32,1,128]{3,1,2,0:T(8,128)S(1)} collective-permute-done((f32[18,32,1,128]{3,1,2,0:T(8,128)S(1)}, f32[18,32,1,128]{3,1,2,0:T(8,128)S(1)}, u32[]{:S(2)}, u32[]{:S(2)}) %collective-permute-start.2) | collective-permute-done | bytes 294944 | tf_op jit(solution)/shard_map/ppermute | solution.py:13
  42.7 1.9 %fusion.25 = f32[18,32,8,128]{3,1,2,0:T(8,128)S(1)} fusion(f32[18,32,7,128]{3,1,2,0:T(8,128)S(1)} %fusion.40, f32[18,32,1,128]{3,1,2,0:T(8,128)S(1)} %collective-permute-done.2, f32[18,32,8,127]{3,1,2,0:T(8,128)S(1)} %get-tuple-element.31, f32[18,32,8,127]{3,1,2,0:T(8,128)S(1)} %get-tuple-element.30, f32[9,32,8,128]{3,1,2,0:T(8,128)S(1)} %get-tuple-element.18, ...), kind=kLoop, calls=%fused_computation.54 | loop fusion | flops 8257536 | bytes 11768832 | tf_op jit(solution)/shard_map/add | solution.py:41
  44.9 1.8 %fusion.29 = f32[18,32,8,128]{3,1,2,0:T(8,128)S(1)} fusion(f32[18,32,1,128]{3,1,2,0:T(8,128)S(1)} %collective-permute-done.3, f32[18,32,7,128]{3,1,2,0:T(8,128)S(1)} %slice.250, f32[18,32,8,127]{3,1,2,0:T(8,128)S(1)} %get-tuple-element.17, f32[18,32,8,127]{3,1,2,0:T(8,128)S(1)} %get-tuple-element.16, f32[36,32,8,128]{3,1,2,0:T(8,128)S(1)} %multiply_divide_fusion.2, ...), kind=kLoop, calls=%fused_computation.59 | loop fusion | flops 7667712 | bytes 11768832 | tf_op jit(solution)/shard_map/add | solution.py:41
  46.7 0.6 fusion.6
  47.4 1.4 %multiply_divide_fusion.1 = f32[36,32,8,128]{3,1,2,0:T(8,128)S(1)} fusion(f32[9,32,8,128]{3,1,2,0:T(8,128)S(1)} %get-tuple-element.29, f32[18,32,8,128]{3,1,2,0:T(8,128)S(1)} %fusion.29, f32[9,32,8,128]{3,1,2,0:T(8,128)S(1)} %get-tuple-element.28, f32[32,8,128]{2,0,1:T(8,128)S(1)} %multiply_add_fusion.2, f32[32]{0:T(128)S(1)} %power_multiply_fusion, ...), kind=kLoop, calls=%fused_computation.9 | loop fusion | flops 11796480 | bytes 9719936 | tf_op jit(solution)/shard_map/div | solution.py:58
  48.8 0.9 fusion.55
  49.6 0.3 fusion.56
  50.0 0.2 fusion.39
  50.3 0.2 slice.267
  50.5 4.5 %collective-permute-start.5 = (f32[18,32,1,128]{3,1,2,0:T(8,128)S(1)}, f32[18,32,1,128]{3,1,2,0:T(8,128)S(1)}, u32[]{:S(2)}, u32[]{:S(2)}) collective-permute-start(f32[18,32,1,128]{3,1,2,0:T(8,128)S(1)} %slice.268), channel_id=1, source_target_pairs={{0,15},{1,0},{2,1},{3,2},{4,3},{5,4},{6,5},{7,6},{8,7},{9,8},{10,9... | collective-permute-start | bytes 884744 | tf_op jit(solution)/shard_map/ppermute | solution.py:13
  55.0 0.9 fusion.8
  55.9 3.0 %collective-permute-done.4 = f32[18,32,1,128]{3,1,2,0:T(8,128)S(1)} collective-permute-done((f32[18,32,1,128]{3,1,2,0:T(8,128)S(1)}, f32[18,32,1,128]{3,1,2,0:T(8,128)S(1)}, u32[]{:S(2)}, u32[]{:S(2)}) %collective-permute-start.4) | collective-permute-done | bytes 294944 | tf_op jit(solution)/shard_map/ppermute | solution.py:13
  58.9 1.9 %fusion.34 = f32[18,32,8,128]{3,1,2,0:T(8,128)S(1)} fusion(f32[18,32,7,128]{3,1,2,0:T(8,128)S(1)} %fusion.39, f32[18,32,1,128]{3,1,2,0:T(8,128)S(1)} %collective-permute-done.4, f32[18,32,8,127]{3,1,2,0:T(8,128)S(1)} %get-tuple-element.27, f32[18,32,8,127]{3,1,2,0:T(8,128)S(1)} %get-tuple-element.26, f32[9,32,8,128]{3,1,2,0:T(8,128)S(1)} %get-tuple-element.14, ...), kind=kLoop, calls=%fused_computation.65 | loop fusion | flops 8257536 | bytes 11768832 | tf_op jit(solution)/shard_map/add | solution.py:41
  61.0 1.8 %fusion.38 = f32[18,32,8,128]{3,1,2,0:T(8,128)S(1)} fusion(f32[18,32,1,128]{3,1,2,0:T(8,128)S(1)} %collective-permute-done.5, f32[18,32,7,128]{3,1,2,0:T(8,128)S(1)} %slice.267, f32[18,32,8,127]{3,1,2,0:T(8,128)S(1)} %get-tuple-element.13, f32[18,32,8,127]{3,1,2,0:T(8,128)S(1)} %get-tuple-element.12, f32[36,32,8,128]{3,1,2,0:T(8,128)S(1)} %multiply_divide_fusion.1, ...), kind=kLoop, calls=%fused_computation.70 | loop fusion | flops 7667712 | bytes 11768832 | tf_op jit(solution)/shard_map/add | solution.py:41
  62.8 0.6 fusion.41
  63.5 1.8 %fusion.4 = (f32[36,32,8,128]{3,1,2,0:T(8,128)S(1)}, f32[36,32,8,128]{3,1,2,0:T(8,128)S(1)}) fusion(f32[32]{0:T(128)S(1)} %power_multiply_fusion, f32[36,8,128]{2,1,0:T(8,128)S(1)} %multiply_add_fusion, f32[8,128]{1,0:T(8,128)S(1)} %convert_element_type.3, f32[9,32,8,128]{3,1,2,0:T(8,128)S(1)} %get-tuple-element.25, f32[18,32,8,128]{3,1,2,0:T(8,128)S(1)} %fusion.38, ...), kind=kLoop, calls=%fused_computation.12 | loop fusion | flops 12976128 | bytes 14438528 | tf_op jit(solution)/shard_map/mul | solution.py:58
  65.3 6.5 %copy.39 = f32[36,32,8,128]{3,2,1,0:T(8,128)} copy(f32[36,32,8,128]{3,1,2,0:T(8,128)S(1)} %get-tuple-element.11) | data formatting | bytes 9437184
  71.8 2.4 %fusion.45 = f32[2,8,128]{2,0,1:T(2,128)S(1)} fusion(f32[2,36,32,1]{2,0,1,3:T(2,128)S(1)} %copy.41, f32[36,32,8,128]{3,1,2,0:T(8,128)S(1)} %get-tuple-element.11), kind=kOutput, calls=%fused_computation.77 | convolution fusion | flops 28311552 | bytes 4736000 | tf_op jit(solution)/shard_map/cij,ijxy->cxy/dot_general | solution.py:63
  74.2 2.4 %fusion.42 = f32[2,8,128]{2,0,1:T(2,128)S(1)} fusion(f32[2,36,32,1]{2,0,1,3:T(2,128)S(1)} %copy.41, f32[36,32,8,128]{3,1,2,0:T(8,128)S(1)} %get-tuple-element.10), kind=kOutput, calls=%fused_computation.76 | convolution fusion | flops 28311552 | bytes 4736000 | tf_op jit(solution)/shard_map/cij,ijxy->cxy/dot_general | solution.py:62
  76.8 0.8 gather_fusion
  77.6 17.9 %all_gather.3 = f32[4,128,128]{1,0,2:T(4,128)S(1)} all-gather(f32[4,128,8]{1,0,2:T(4,128)S(1)} %copy.38), channel_id=1, replica_groups=mesh['member'=2,'gx'=16] {'gx'}, dimensions={2}, use_global_device_ids=true | all-gather | bytes 278528 | tf_op jit(solution)/shard_map/all_gather | solution.py:89
  95.7 0.7 copy.40
  (57 shorter events, 2.3 us)
Async XLA Ops:
  2.4 2.4 %copy-start = (f32[36,32,8,128]{3,2,1,0:T(8,128)S(1)}, f32[36,32,8,128]{3,2,1,0:T(8,128)}, u32[]{:S(2)}) copy-start(f32[36,32,8,128]{3,2,1,0:T(8,128)} %param.4) | copy-start | bytes 14155780
  3.6 18.8 %collective-permute-start = (f32[18,32,1,128]{3,1,2,0:T(8,128)}, f32[18,32,1,128]{3,1,2,0:T(8,128)S(1)}, u32[]{:S(2)}, u32[]{:S(2)}) collective-permute-start(f32[18,32,1,128]{3,1,2,0:T(8,128)} %slice.228), channel_id=1, source_target_pairs={{0,1},{1,2},{2,3},{3,4},{4,5},{5,6},{6,7},{7,8},{8,9},{9,10},{10,1... | collective-permute-start | bytes 884744 | tf_op jit(solution)/shard_map/ppermute | solution.py:13
  5.1 21.7 %collective-permute-start.1 = (f32[18,32,1,128]{3,1,2,0:T(8,128)S(1)}, f32[18,32,1,128]{3,1,2,0:T(8,128)S(1)}, u32[]{:S(2)}, u32[]{:S(2)}) collective-permute-start(f32[18,32,1,128]{3,1,2,0:T(8,128)S(1)} %bitcast.18), channel_id=1, source_target_pairs={{0,15},{1,0},{2,1},{3,2},{4,3},{5,4},{6,5},{7,6},{8,7},{9,8},{10,9... | collective-permute-start | bytes 884744 | tf_op jit(solution)/shard_map/ppermute | solution.py:13
  20.3 1.7 %copy-start.5 = (s32[8,128]{1,0:T(8,128)S(1)}, s32[8,128]{1,0:T(8,128)}, u32[]{:S(2)}) copy-start(s32[8,128]{1,0:T(8,128)} %param.6) | copy-start | bytes 12292
  20.3 1.7 %copy-start.4 = (f32[2,8,128]{2,1,0:T(8,128)S(1)}, f32[2,8,128]{2,1,0:T(8,128)}, u32[]{:S(2)}) copy-start(f32[2,8,128]{2,1,0:T(8,128)} %param.5) | copy-start | bytes 24580
  20.3 1.9 %copy-start.6 = (s32[128]{0:T(128)S(1)}, s32[128]{0:T(128)}, u32[]{:S(2)}) copy-start(s32[128]{0:T(128)} %param.7) | copy-start | bytes 1540
  22.4 4.3 %copy-start.2 = (f32[18,32,8,127]{3,1,2,0:T(8,128)S(1)}, f32[18,32,8,127]{3,1,2,0:T(8,128)}, u32[]{:S(2)}) copy-start(f32[18,32,8,127]{3,1,2,0:T(8,128)} %copy.59) | copy-start | bytes 7022596
  22.4 4.3 %copy-start.3 = (f32[18,32,7,128]{3,1,2,0:T(8,128)S(1)}, f32[18,32,7,128]{3,1,2,0:T(8,128)}, u32[]{:S(2)}) copy-start(f32[18,32,7,128]{3,1,2,0:T(8,128)} %copy.56) | copy-start | bytes 6193156
  26.4 1.7 %slice-start = ((f32[36,32,8,128]{3,2,1,0:T(8,128)}), f32[18,32,8,128]{3,2,1,0:T(8,128)S(1)}, s32[]{:S(2)}) async-start(f32[36,32,8,128]{3,2,1,0:T(8,128)} %param.4), calls=%async_computation | async-start | bytes 4718592 | tf_op jit(solution)/shard_map/slice | solution.py:78
  26.4 2.4 %copy-start.1 = (f32[18,32,8,127]{3,1,2,0:T(8,128)S(1)}, f32[18,32,8,127]{3,1,2,0:T(8,128)}, u32[]{:S(2)}) copy-start(f32[18,32,8,127]{3,1,2,0:T(8,128)} %copy.58) | copy-start | bytes 7022596
  33.8 8.9 %collective-permute-start.2 = (f32[18,32,1,128]{3,1,2,0:T(8,128)S(1)}, f32[18,32,1,128]{3,1,2,0:T(8,128)S(1)}, u32[]{:S(2)}, u32[]{:S(2)}) collective-permute-start(f32[18,32,1,128]{3,1,2,0:T(8,128)S(1)} %fusion.49), channel_id=1, source_target_pairs={{0,1},{1,2},{2,3},{3,4},{4,5},{5,6},{6,7},{7,8},{8,9},{9,10},{10,1... | collective-permute-start | bytes 884744 | tf_op jit(solution)/shard_map/ppermute | solution.py:13
  34.4 10.5 %collective-permute-start.3 = (f32[18,32,1,128]{3,1,2,0:T(8,128)S(1)}, f32[18,32,1,128]{3,1,2,0:T(8,128)S(1)}, u32[]{:S(2)}, u32[]{:S(2)}) collective-permute-start(f32[18,32,1,128]{3,1,2,0:T(8,128)S(1)} %slice.251), channel_id=1, source_target_pairs={{0,15},{1,0},{2,1},{3,2},{4,3},{5,4},{6,5},{7,6},{8,7},{9,8},{10,9... | collective-permute-start | bytes 884744 | tf_op jit(solution)/shard_map/ppermute | solution.py:13
  50.0 8.9 %collective-permute-start.4 = (f32[18,32,1,128]{3,1,2,0:T(8,128)S(1)}, f32[18,32,1,128]{3,1,2,0:T(8,128)S(1)}, u32[]{:S(2)}, u32[]{:S(2)}) collective-permute-start(f32[18,32,1,128]{3,1,2,0:T(8,128)S(1)} %fusion.48), channel_id=1, source_target_pairs={{0,1},{1,2},{2,3},{3,4},{4,5},{5,6},{6,7},{7,8},{8,9},{9,10},{10,1... | collective-permute-start | bytes 884744 | tf_op jit(solution)/shard_map/ppermute | solution.py:13
  50.5 10.5 %collective-permute-start.5 = (f32[18,32,1,128]{3,1,2,0:T(8,128)S(1)}, f32[18,32,1,128]{3,1,2,0:T(8,128)S(1)}, u32[]{:S(2)}, u32[]{:S(2)}) collective-permute-start(f32[18,32,1,128]{3,1,2,0:T(8,128)S(1)} %slice.268), channel_id=1, source_target_pairs={{0,15},{1,0},{2,1},{3,2},{4,3},{5,4},{6,5},{7,6},{8,7},{9,8},{10,9... | collective-permute-start | bytes 884744 | tf_op jit(solution)/shard_map/ppermute | solution.py:13
where the time goes:
time: 96.6 us; the launch traced here: 96.4 us
  local copies, waits for them, and re-layouts  29.2 us (30%)
  other arithmetic  22.3 us (23%)
  blocking collectives  17.9 us (19%)
  starting transfers between devices  15.3 us (16%)
  waiting for transfers between devices  5.77 us (6%)
  matrix products  4.79 us (5%)
  between operations  1.14 us (1%)
    all_gather x1, blocking collectives, per_device(): gathered = lax.all_gather(local_rows, 'gx', axis=2, tiled=True)  17.9 us
    ppermute x6, starting transfers between devices, passed_along(): return lax.ppermute(value, axis, pairs)  15.3 us
    unnamed x20, local copies, waits for them, and re-layouts  14.3 us
    add x6, other arithmetic, upwind(): center - jnp.maximum(along_x, 0.0) * (center - west_cell)  13.1 us
    ppermute x6, waiting for transfers between devices, passed_along(): return lax.ppermute(value, axis, pairs)  5.77 us
    slice x4, local copies, waits for them, and re-layouts, upwind(): south_cell = jnp.concatenate([border, center[..., :-1]], axis=3)  5.63 us
    div x2, other arithmetic, sources(): return (advected * (1.0 + growth) / (1.0 + damping), growth * advected)  2.77 us
    dot_general x1, matrix products, coupling_fields(): jnp.einsum('cij,ijxy->cxy', project, input_flux, precision=lax.Precision....  2.41 us
  transfers between devices with their start and end apart: 6, of which 2 were waited for; matrix products, arithmetic and copies ran while one was open for 24% of the time, Pallas kernels for 0%

commit v1 on v0

--- a/solution.py
+++ b/solution.py
@@ -65,6 +65,24 @@
 
 
 def per_device(spectrum, wind, land_sea, band_rows):
+
+    def form_the_cards(panel):
+        n_lanes = lax.psum(1, "gx")
+        r1 = range(n_lanes)
+        u_next = map(lambda nth: (nth, (nth + 1) % n_lanes), r1)
+        entries = list(u_next)
+
+        def save_ends(m_next):
+            if len(m_next) == n_lanes:
+                return m_next
+            far_arr = lax.ppermute(m_next[0], "gx", entries)
+            return save_ends([far_arr, *m_next])
+
+        u1 = save_ends([panel])
+        state_now = jnp.concatenate(u1, axis=2)
+        step_out = lax.axis_index("gx")
+        return jnp.roll(state_now, (step_out + 1) * panel.shape[2], axis=2)
+
     tables = wave_tables(spectrum.shape[0], spectrum.shape[1])
     sea_mask = land_sea.astype(jnp.float32)
     current = spectrum
@@ -86,7 +104,7 @@
         current, input_flux = sources(advected, wind[0], wind[1], sea_mask, tables)
     fields = coupling_fields(input_flux, current, tables[6])
     local_rows = jnp.transpose(fields[:, :, band_rows], (0, 2, 1))
-    gathered = lax.all_gather(local_rows, "gx", axis=2, tiled=True)
+    gathered = form_the_cards(local_rows)
     band_count = local_rows.shape[1] // lax.axis_size("gx")
     ocean_fields = lax.dynamic_slice_in_dim(
         gathered, lax.axis_index("gx") * band_count, band_count, 1

time: 96.6 us -> 215 us (2.23)
  waiting for transfers between devices: 5.77 us -> 125 us
  blocking collectives: 17.9 us -> 0 us
  local copies, waits for them, and re-layouts: 29.2 us -> 46.8 us
    ppermute x0 -> x15, waiting for transfers between devices: none -> 119 us  [save_ends(): far_arr = lax.ppermute(m_next[0], 'gx', entries)]
    all_gather x1 -> x0, blocking collectives: 17.9 us -> none  [per_device(): gathered = lax.all_gather(local_rows, 'gx', axis=2, tiled=True)]
    concatenate x0 -> x1, local copies, waits for them, and re-layouts: none -> 14.1 us  [form_the_cards(): return jnp.roll(state_now, (step_out + 1) * panel.shape[2], axis=2)]
    unnamed x20 -> x24, local copies, waits for them, and re-layouts: 14.3 us -> 17.2 us
  transfers between devices with their start and end apart: 6 -> 21, of which waited for: 2 -> 16; matrix products, arithmetic and copies ran while one was open for 24% -> 15% of each run, Pallas kernels for 0% -> 0%
where the time goes in v1:
time: 215 us
  waiting for transfers between devices  125 us (58%)
  local copies, waits for them, and re-layouts  46.8 us (22%)
  other arithmetic  22.1 us (10%)
  starting transfers between devices  15.6 us (7%)
  matrix products  4.8 us (2%)
    ppermute x15, waiting for transfers between devices, save_ends(): far_arr = lax.ppermute(m_next[0], 'gx', entries)  119 us
    unnamed x24, local copies, waits for them, and re-layouts  17.2 us
    ppermute x6, starting transfers between devices, passed_along(): return lax.ppermute(value, axis, pairs)  15.5 us
    concatenate x1, local copies, waits for them, and re-layouts, form_the_cards(): return jnp.roll(state_now, (step_out + 1) * panel.shape[2], axis=2)  14.1 us
    add x6, other arithmetic, upwind(): center - jnp.maximum(along_x, 0.0) * (center - west_cell)  13.1 us
    slice x4, local copies, waits for them, and re-layouts, upwind(): south_cell = jnp.concatenate([border, center[..., :-1]], axis=3)  5.63 us
    ppermute x6, waiting for transfers between devices, passed_along(): return lax.ppermute(value, axis, pairs)  5.55 us
  transfers between devices with their start and end apart: 21, of which 16 were waited for; matrix products, arithmetic and copies ran while one was open for 15% of the time, Pallas kernels for 0%

profile of v1, /device:TPU:0, one launch (start us, length us, event | category | flops | bytes accessed | tf_op | source)
XLA Modules:
  0.0 215.0 jit_solution(11694411466555159869)
XLA Ops:
  0.6 1.8 fusion.60
  2.9 0.7 slice.228
  4.1 0.8 copy-done.1
  5.1 5.5 %collective-permute-start.1 = (f32[18,32,1,128]{3,1,2,0:T(8,128)S(1)}, f32[18,32,1,128]{3,1,2,0:T(8,128)S(1)}, u32[]{:S(2)}, u32[]{:S(2)}) collective-permute-start(f32[18,32,1,128]{3,1,2,0:T(8,128)S(1)} %bitcast.20), channel_id=1, source_target_pairs={{0,15},{1,0},{2,1},{3,2},{4,3},{5,4},{6,5},{7,6},{8,7},{9,8},{10,9... | collective-permute-start | bytes 884744 | tf_op jit(solution)/shard_map/ppermute | solution.py:13
  10.6 3.1 %fusion.64 = (f32[18,32,8,127]{3,1,2,0:T(8,128)}, f32[18,32,8,127]{3,1,2,0:T(8,128)}) fusion(f32[18,32,8,128]{3,1,2,0:T(8,128)S(1)} %copy_dynamic-update-slice_fusion), kind=kLoop, calls=%fused_computation.125 | loop fusion | bytes 9363456 | tf_op jit(solution)/shard_map/slice | solution.py:38
  13.7 1.6 slice.229
  15.5 0.8 fusion.59
  16.6 1.8 copy.56
  18.5 1.8 copy.57
  20.3 1.7 copy.54
  22.4 4.0 %fusion.16 = f32[18,32,8,128]{3,1,2,0:T(8,128)S(1)} fusion(f32[18,32,8,128]{3,1,2,0:T(8,128)S(1)} %copy_dynamic-update-slice_fusion, f32[18,32,7,128]{3,1,2,0:T(8,128)} %slice.229, f32[18,32,1,128]{3,1,2,0:T(8,128)S(1)} %collective-permute-done, f32[18,32,8,127]{3,1,2,0:T(8,128)} %get-tuple-element.35, f32[18,32,8,127]{3,1,2,0:T(8,128)} %get-tuple-element.34, ...), kind=kLoop, calls=%fused_computation.43 | loop fusion | flops 7667712 | bytes 11768832 | tf_op jit(solution)/shard_map/add | solution.py:41
  26.7 1.4 slice-done
  28.8 1.7 fusion.20
  31.2 1.4 multiply_divide_fusion.2
  32.6 0.9 fusion.57
  34.4 4.7 %collective-permute-start.3 = (f32[18,32,1,128]{3,1,2,0:T(8,128)S(1)}, f32[18,32,1,128]{3,1,2,0:T(8,128)S(1)}, u32[]{:S(2)}, u32[]{:S(2)}) collective-permute-start(f32[18,32,1,128]{3,1,2,0:T(8,128)S(1)} %slice.251), channel_id=1, source_target_pairs={{0,15},{1,0},{2,1},{3,2},{4,3},{5,4},{6,5},{7,6},{8,7},{9,8},{10,9... | collective-permute-start | bytes 884744 | tf_op jit(solution)/shard_map/ppermute | solution.py:13
  39.1 0.9 fusion.10
  39.9 2.8 %collective-permute-done.2 = f32[18,32,1,128]{3,1,2,0:T(8,128)S(1)} collective-permute-done((f32[18,32,1,128]{3,1,2,0:T(8,128)S(1)}, f32[18,32,1,128]{3,1,2,0:T(8,128)S(1)}, u32[]{:S(2)}, u32[]{:S(2)}) %collective-permute-start.2) | collective-permute-done | bytes 294944 | tf_op jit(solution)/shard_map/ppermute | solution.py:13
  42.7 1.9 fusion.25
  44.9 1.8 fusion.29
  47.4 1.4 multiply_divide_fusion.1
  48.8 0.9 fusion.55
  50.5 4.7 %collective-permute-start.5 = (f32[18,32,1,128]{3,1,2,0:T(8,128)S(1)}, f32[18,32,1,128]{3,1,2,0:T(8,128)S(1)}, u32[]{:S(2)}, u32[]{:S(2)}) collective-permute-start(f32[18,32,1,128]{3,1,2,0:T(8,128)S(1)} %slice.268), channel_id=1, source_target_pairs={{0,15},{1,0},{2,1},{3,2},{4,3},{5,4},{6,5},{7,6},{8,7},{9,8},{10,9... | collective-permute-start | bytes 884744 | tf_op jit(solution)/shard_map/ppermute | solution.py:13
  55.2 0.9 fusion.8
  56.1 2.8 %collective-permute-done.4 = f32[18,32,1,128]{3,1,2,0:T(8,128)S(1)} collective-permute-done((f32[18,32,1,128]{3,1,2,0:T(8,128)S(1)}, f32[18,32,1,128]{3,1,2,0:T(8,128)S(1)}, u32[]{:S(2)}, u32[]{:S(2)}) %collective-permute-start.4) | collective-permute-done | bytes 294944 | tf_op jit(solution)/shard_map/ppermute | solution.py:13
  58.8 1.9 fusion.34
  61.0 1.8 fusion.38
  63.5 1.6 fusion.4
  65.0 2.4 %fusion.42 = f32[2,8,128]{2,0,1:T(2,128)S(1)} fusion(f32[2,36,32,1]{2,0,1,3:T(2,128)S(1)} %copy.39, f32[36,32,8,128]{3,1,2,0:T(8,128)S(1)} %get-tuple-element.10), kind=kOutput, calls=%fused_computation.76 | convolution fusion | flops 28311552 | bytes 4736000 | tf_op jit(solution)/shard_map/cij,ijxy->cxy/dot_general | solution.py:62
  67.4 2.4 %fusion.45 = f32[2,8,128]{2,0,1:T(2,128)S(1)} fusion(f32[2,36,32,1]{2,0,1,3:T(2,128)S(1)} %copy.39, f32[36,32,8,128]{3,1,2,0:T(8,128)S(1)} %get-tuple-element.11), kind=kOutput, calls=%fused_computation.77 | convolution fusion | flops 28311552 | bytes 4736000 | tf_op jit(solution)/shard_map/cij,ijxy->cxy/dot_general | solution.py:63
  70.0 0.8 gather_fusion
  70.9 8.5 %collective-permute-done.6 = f32[4,128,8]{2,0,1:T(4,128)S(1)} collective-permute-done((f32[4,128,8]{2,0,1:T(4,128)S(1)}, f32[4,128,8]{2,0,1:T(4,128)S(1)}, u32[]{:S(2)}, u32[]{:S(2)}) %collective-permute-start.6) | collective-permute-done | bytes 16416 | tf_op jit(solution)/shard_map/ppermute | solution.py:78
  79.3 8.5 %collective-permute-done.7 = f32[4,128,8]{2,0,1:T(4,128)S(1)} collective-permute-done((f32[4,128,8]{2,0,1:T(4,128)S(1)}, f32[4,128,8]{2,0,1:T(4,128)S(1)}, u32[]{:S(2)}, u32[]{:S(2)}) %collective-permute-start.7) | collective-permute-done | bytes 16416 | tf_op jit(solution)/shard_map/ppermute | solution.py:78
  87.8 8.5 %collective-permute-done.8 = f32[4,128,8]{2,0,1:T(4,128)S(1)} collective-permute-done((f32[4,128,8]{2,0,1:T(4,128)S(1)}, f32[4,128,8]{2,0,1:T(4,128)S(1)}, u32[]{:S(2)}, u32[]{:S(2)}) %collective-permute-start.8) | collective-permute-done | bytes 16416 | tf_op jit(solution)/shard_map/ppermute | solution.py:78
  96.3 8.5 %collective-permute-done.9 = f32[4,128,8]{2,0,1:T(4,128)S(1)} collective-permute-done((f32[4,128,8]{2,0,1:T(4,128)S(1)}, f32[4,128,8]{2,0,1:T(4,128)S(1)}, u32[]{:S(2)}, u32[]{:S(2)}) %collective-permute-start.9) | collective-permute-done | bytes 16416 | tf_op jit(solution)/shard_map/ppermute | solution.py:78
  104.8 8.5 %collective-permute-done.10 = f32[4,128,8]{2,0,1:T(4,128)S(1)} collective-permute-done((f32[4,128,8]{2,0,1:T(4,128)S(1)}, f32[4,128,8]{2,0,1:T(4,128)S(1)}, u32[]{:S(2)}, u32[]{:S(2)}) %collective-permute-start.10) | collective-permute-done | bytes 16416 | tf_op jit(solution)/shard_map/ppermute | solution.py:78
  113.3 8.5 %collective-permute-done.11 = f32[4,128,8]{2,0,1:T(4,128)S(1)} collective-permute-done((f32[4,128,8]{2,0,1:T(4,128)S(1)}, f32[4,128,8]{2,0,1:T(4,128)S(1)}, u32[]{:S(2)}, u32[]{:S(2)}) %collective-permute-start.11) | collective-permute-done | bytes 16416 | tf_op jit(solution)/shard_map/ppermute | solution.py:78
  121.8 8.5 %collective-permute-done.12 = f32[4,128,8]{2,0,1:T(4,128)S(1)} collective-permute-done((f32[4,128,8]{2,0,1:T(4,128)S(1)}, f32[4,128,8]{2,0,1:T(4,128)S(1)}, u32[]{:S(2)}, u32[]{:S(2)}) %collective-permute-start.12) | collective-permute-done | bytes 16416 | tf_op jit(solution)/shard_map/ppermute | solution.py:78
  130.3 8.5 %collective-permute-done.13 = f32[4,128,8]{2,0,1:T(4,128)S(1)} collective-permute-done((f32[4,128,8]{2,0,1:T(4,128)S(1)}, f32[4,128,8]{2,0,1:T(4,128)S(1)}, u32[]{:S(2)}, u32[]{:S(2)}) %collective-permute-start.13) | collective-permute-done | bytes 16416 | tf_op jit(solution)/shard_map/ppermute | solution.py:78
  138.8 8.5 %collective-permute-done.14 = f32[4,128,8]{2,0,1:T(4,128)S(1)} collective-permute-done((f32[4,128,8]{2,0,1:T(4,128)S(1)}, f32[4,128,8]{2,0,1:T(4,128)S(1)}, u32[]{:S(2)}, u32[]{:S(2)}) %collective-permute-start.14) | collective-permute-done | bytes 16416 | tf_op jit(solution)/shard_map/ppermute | solution.py:78
  147.3 8.5 %collective-permute-done.15 = f32[4,128,8]{2,0,1:T(4,128)S(1)} collective-permute-done((f32[4,128,8]{2,0,1:T(4,128)S(1)}, f32[4,128,8]{2,0,1:T(4,128)S(1)}, u32[]{:S(2)}, u32[]{:S(2)}) %collective-permute-start.15) | collective-permute-done | bytes 16416 | tf_op jit(solution)/shard_map/ppermute | solution.py:78
  155.8 8.5 %collective-permute-done.16 = f32[4,128,8]{2,0,1:T(4,128)S(1)} collective-permute-done((f32[4,128,8]{2,0,1:T(4,128)S(1)}, f32[4,128,8]{2,0,1:T(4,128)S(1)}, u32[]{:S(2)}, u32[]{:S(2)}) %collective-permute-start.16) | collective-permute-done | bytes 16416 | tf_op jit(solution)/shard_map/ppermute | solution.py:78
  164.3 8.5 %collective-permute-done.17 = f32[4,128,8]{2,0,1:T(4,128)S(1)} collective-permute-done((f32[4,128,8]{2,0,1:T(4,128)S(1)}, f32[4,128,8]{2,0,1:T(4,128)S(1)}, u32[]{:S(2)}, u32[]{:S(2)}) %collective-permute-start.17) | collective-permute-done | bytes 16416 | tf_op jit(solution)/shard_map/ppermute | solution.py:78
  172.8 8.5 %collective-permute-done.18 = f32[4,128,8]{2,0,1:T(4,128)S(1)} collective-permute-done((f32[4,128,8]{2,0,1:T(4,128)S(1)}, f32[4,128,8]{2,0,1:T(4,128)S(1)}, u32[]{:S(2)}, u32[]{:S(2)}) %collective-permute-start.18) | collective-permute-done | bytes 16416 | tf_op jit(solution)/shard_map/ppermute | solution.py:78
  182.0 8.6 %collective-permute-done.19 = f32[4,128,8]{2,0,1:T(4,128)} collective-permute-done((f32[4,128,8]{2,0,1:T(4,128)S(1)}, f32[4,128,8]{2,0,1:T(4,128)}, u32[]{:S(2)}, u32[]{:S(2)}) %collective-permute-start.19) | collective-permute-done | bytes 16416 | tf_op jit(solution)/shard_map/ppermute | solution.py:78
  190.6 8.9 %copy.37 = f32[36,32,8,128]{3,2,1,0:T(8,128)} copy(f32[36,32,8,128]{3,1,2,0:T(8,128)} %copy-done) | data formatting | bytes 9437184
  199.4 14.1 %concatenate.130 = f32[4,128,256]{2,0,1:T(4,128)} concatenate(f32[4,128,8]{2,0,1:T(4,128)} %collective-permute-done.20, f32[4,128,8]{2,0,1:T(4,128)} %collective-permute-done.19, f32[4,128,8]{2,0,1:T(4,128)} %copy-done.5, f32[4,128,8]{2,0,1:T(4,128)S(1)} %collective-permute-done.17, f32[4,128,8]{2,0,1:T(4,128)S(1)} %collective-permute-done.16, ...), dimensions={2} | concatenate | bytes 1048576 | tf_op jit(solution)/shard_map/jit(_roll_dynamic)/concatenate | solution.py:84
  213.6 0.8 constant_dynamic-slice_fusion
  (90 shorter events, 8.7 us)
Async XLA Ops:
  2.4 2.4 %copy-start.1 = (f32[36,32,8,128]{3,2,1,0:T(8,128)S(1)}, f32[36,32,8,128]{3,2,1,0:T(8,128)}, u32[]{:S(2)}) copy-start(f32[36,32,8,128]{3,2,1,0:T(8,128)} %param.4) | copy-start | bytes 14155780
  3.6 18.8 %collective-permute-start = (f32[18,32,1,128]{3,1,2,0:T(8,128)}, f32[18,32,1,128]{3,1,2,0:T(8,128)S(1)}, u32[]{:S(2)}, u32[]{:S(2)}) collective-permute-start(f32[18,32,1,128]{3,1,2,0:T(8,128)} %slice.228), channel_id=1, source_target_pairs={{0,1},{1,2},{2,3},{3,4},{4,5},{5,6},{6,7},{7,8},{8,9},{9,10},{10,1... | collective-permute-start | bytes 884744 | tf_op jit(solution)/shard_map/ppermute | solution.py:13
  5.1 21.7 %collective-permute-start.1 = (f32[18,32,1,128]{3,1,2,0:T(8,128)S(1)}, f32[18,32,1,128]{3,1,2,0:T(8,128)S(1)}, u32[]{:S(2)}, u32[]{:S(2)}) collective-permute-start(f32[18,32,1,128]{3,1,2,0:T(8,128)S(1)} %bitcast.20), channel_id=1, source_target_pairs={{0,15},{1,0},{2,1},{3,2},{4,3},{5,4},{6,5},{7,6},{8,7},{9,8},{10,9... | collective-permute-start | bytes 884744 | tf_op jit(solution)/shard_map/ppermute | solution.py:13
  20.3 1.7 copy-start.7
  20.3 1.7 copy-start.6
  20.3 1.9 copy-start.8
  22.4 4.3 %copy-start.3 = (f32[18,32,8,127]{3,1,2,0:T(8,128)S(1)}, f32[18,32,8,127]{3,1,2,0:T(8,128)}, u32[]{:S(2)}) copy-start(f32[18,32,8,127]{3,1,2,0:T(8,128)} %copy.57) | copy-start | bytes 7022596
  22.4 4.3 %copy-start.4 = (f32[18,32,7,128]{3,1,2,0:T(8,128)S(1)}, f32[18,32,7,128]{3,1,2,0:T(8,128)}, u32[]{:S(2)}) copy-start(f32[18,32,7,128]{3,1,2,0:T(8,128)} %copy.54) | copy-start | bytes 6193156
  26.4 1.7 slice-start
  26.4 2.4 %copy-start.2 = (f32[18,32,8,127]{3,1,2,0:T(8,128)S(1)}, f32[18,32,8,127]{3,1,2,0:T(8,128)}, u32[]{:S(2)}) copy-start(f32[18,32,8,127]{3,1,2,0:T(8,128)} %copy.56) | copy-start | bytes 7022596
  33.8 8.9 %collective-permute-start.2 = (f32[18,32,1,128]{3,1,2,0:T(8,128)S(1)}, f32[18,32,1,128]{3,1,2,0:T(8,128)S(1)}, u32[]{:S(2)}, u32[]{:S(2)}) collective-permute-start(f32[18,32,1,128]{3,1,2,0:T(8,128)S(1)} %fusion.49), channel_id=1, source_target_pairs={{0,1},{1,2},{2,3},{3,4},{4,5},{5,6},{6,7},{7,8},{8,9},{9,10},{10,1... | collective-permute-start | bytes 884744 | tf_op jit(solution)/shard_map/ppermute | solution.py:13
  34.4 10.5 %collective-permute-start.3 = (f32[18,32,1,128]{3,1,2,0:T(8,128)S(1)}, f32[18,32,1,128]{3,1,2,0:T(8,128)S(1)}, u32[]{:S(2)}, u32[]{:S(2)}) collective-permute-start(f32[18,32,1,128]{3,1,2,0:T(8,128)S(1)} %slice.251), channel_id=1, source_target_pairs={{0,15},{1,0},{2,1},{3,2},{4,3},{5,4},{6,5},{7,6},{8,7},{9,8},{10,9... | collective-permute-start | bytes 884744 | tf_op jit(solution)/shard_map/ppermute | solution.py:13
  49.9 8.9 %collective-permute-start.4 = (f32[18,32,1,128]{3,1,2,0:T(8,128)S(1)}, f32[18,32,1,128]{3,1,2,0:T(8,128)S(1)}, u32[]{:S(2)}, u32[]{:S(2)}) collective-permute-start(f32[18,32,1,128]{3,1,2,0:T(8,128)S(1)} %fusion.48), channel_id=1, source_target_pairs={{0,1},{1,2},{2,3},{3,4},{4,5},{5,6},{6,7},{7,8},{8,9},{9,10},{10,1... | collective-permute-start | bytes 884744 | tf_op jit(solution)/shard_map/ppermute | solution.py:13
  50.5 10.5 %collective-permute-start.5 = (f32[18,32,1,128]{3,1,2,0:T(8,128)S(1)}, f32[18,32,1,128]{3,1,2,0:T(8,128)S(1)}, u32[]{:S(2)}, u32[]{:S(2)}) collective-permute-start(f32[18,32,1,128]{3,1,2,0:T(8,128)S(1)} %slice.268), channel_id=1, source_target_pairs={{0,15},{1,0},{2,1},{3,2},{4,3},{5,4},{6,5},{7,6},{8,7},{9,8},{10,9... | collective-permute-start | bytes 884744 | tf_op jit(solution)/shard_map/ppermute | solution.py:13
  65.0 2.4 %copy-start = (f32[36,32,8,128]{3,1,2,0:T(8,128)}, f32[36,32,8,128]{3,1,2,0:T(8,128)S(1)}, u32[]{:S(2)}) copy-start(f32[36,32,8,128]{3,1,2,0:T(8,128)S(1)} %get-tuple-element.11) | copy-start | bytes 14155780
  70.8 8.5 %collective-permute-start.6 = (f32[4,128,8]{2,0,1:T(4,128)S(1)}, f32[4,128,8]{2,0,1:T(4,128)S(1)}, u32[]{:S(2)}, u32[]{:S(2)}) collective-permute-start(f32[4,128,8]{2,0,1:T(4,128)S(1)} %bitcast.17), channel_id=1, source_target_pairs={{0,1},{1,2},{2,3},{3,4},{4,5},{5,6},{6,7},{7,8},{8,9},{9,10},{10,1... | collective-permute-start | bytes 49160 | tf_op jit(solution)/shard_map/ppermute | solution.py:78
  79.3 8.5 %collective-permute-start.7 = (f32[4,128,8]{2,0,1:T(4,128)S(1)}, f32[4,128,8]{2,0,1:T(4,128)S(1)}, u32[]{:S(2)}, u32[]{:S(2)}) collective-permute-start(f32[4,128,8]{2,0,1:T(4,128)S(1)} %collective-permute-done.6), channel_id=1, source_target_pairs={{0,1},{1,2},{2,3},{3,4},{4,5},{5,6},{6,7},{7,8},{8,9},{9,10},{10,1... | collective-permute-start | bytes 49160 | tf_op jit(solution)/shard_map/ppermute | solution.py:78
  87.8 8.5 %collective-permute-start.8 = (f32[4,128,8]{2,0,1:T(4,128)S(1)}, f32[4,128,8]{2,0,1:T(4,128)S(1)}, u32[]{:S(2)}, u32[]{:S(2)}) collective-permute-start(f32[4,128,8]{2,0,1:T(4,128)S(1)} %collective-permute-done.7), channel_id=1, source_target_pairs={{0,1},{1,2},{2,3},{3,4},{4,5},{5,6},{6,7},{7,8},{8,9},{9,10},{10,1... | collective-permute-start | bytes 49160 | tf_op jit(solution)/shard_map/ppermute | solution.py:78
  96.3 8.5 %collective-permute-start.9 = (f32[4,128,8]{2,0,1:T(4,128)S(1)}, f32[4,128,8]{2,0,1:T(4,128)S(1)}, u32[]{:S(2)}, u32[]{:S(2)}) collective-permute-start(f32[4,128,8]{2,0,1:T(4,128)S(1)} %collective-permute-done.8), channel_id=1, source_target_pairs={{0,1},{1,2},{2,3},{3,4},{4,5},{5,6},{6,7},{7,8},{8,9},{9,10},{10,1... | collective-permute-start | bytes 49160 | tf_op jit(solution)/shard_map/ppermute | solution.py:78
  104.8 8.5 %collective-permute-start.10 = (f32[4,128,8]{2,0,1:T(4,128)S(1)}, f32[4,128,8]{2,0,1:T(4,128)S(1)}, u32[]{:S(2)}, u32[]{:S(2)}) collective-permute-start(f32[4,128,8]{2,0,1:T(4,128)S(1)} %collective-permute-done.9), channel_id=1, source_target_pairs={{0,1},{1,2},{2,3},{3,4},{4,5},{5,6},{6,7},{7,8},{8,9},{9,10},{10,1... | collective-permute-start | bytes 49160 | tf_op jit(solution)/shard_map/ppermute | solution.py:78
  113.3 8.5 %collective-permute-start.11 = (f32[4,128,8]{2,0,1:T(4,128)S(1)}, f32[4,128,8]{2,0,1:T(4,128)S(1)}, u32[]{:S(2)}, u32[]{:S(2)}) collective-permute-start(f32[4,128,8]{2,0,1:T(4,128)S(1)} %collective-permute-done.10), channel_id=1, source_target_pairs={{0,1},{1,2},{2,3},{3,4},{4,5},{5,6},{6,7},{7,8},{8,9},{9,10},{10,1... | collective-permute-start | bytes 49160 | tf_op jit(solution)/shard_map/ppermute | solution.py:78
  121.8 8.5 %collective-permute-start.12 = (f32[4,128,8]{2,0,1:T(4,128)S(1)}, f32[4,128,8]{2,0,1:T(4,128)S(1)}, u32[]{:S(2)}, u32[]{:S(2)}) collective-permute-start(f32[4,128,8]{2,0,1:T(4,128)S(1)} %collective-permute-done.11), channel_id=1, source_target_pairs={{0,1},{1,2},{2,3},{3,4},{4,5},{5,6},{6,7},{7,8},{8,9},{9,10},{10,1... | collective-permute-start | bytes 49160 | tf_op jit(solution)/shard_map/ppermute | solution.py:78
  130.3 8.5 %collective-permute-start.13 = (f32[4,128,8]{2,0,1:T(4,128)S(1)}, f32[4,128,8]{2,0,1:T(4,128)S(1)}, u32[]{:S(2)}, u32[]{:S(2)}) collective-permute-start(f32[4,128,8]{2,0,1:T(4,128)S(1)} %collective-permute-done.12), channel_id=1, source_target_pairs={{0,1},{1,2},{2,3},{3,4},{4,5},{5,6},{6,7},{7,8},{8,9},{9,10},{10,1... | collective-permute-start | bytes 49160 | tf_op jit(solution)/shard_map/ppermute | solution.py:78
  138.8 8.5 %collective-permute-start.14 = (f32[4,128,8]{2,0,1:T(4,128)S(1)}, f32[4,128,8]{2,0,1:T(4,128)S(1)}, u32[]{:S(2)}, u32[]{:S(2)}) collective-permute-start(f32[4,128,8]{2,0,1:T(4,128)S(1)} %collective-permute-done.13), channel_id=1, source_target_pairs={{0,1},{1,2},{2,3},{3,4},{4,5},{5,6},{6,7},{7,8},{8,9},{9,10},{10,1... | collective-permute-start | bytes 49160 | tf_op jit(solution)/shard_map/ppermute | solution.py:78
  147.3 8.5 %collective-permute-start.15 = (f32[4,128,8]{2,0,1:T(4,128)S(1)}, f32[4,128,8]{2,0,1:T(4,128)S(1)}, u32[]{:S(2)}, u32[]{:S(2)}) collective-permute-start(f32[4,128,8]{2,0,1:T(4,128)S(1)} %collective-permute-done.14), channel_id=1, source_target_pairs={{0,1},{1,2},{2,3},{3,4},{4,5},{5,6},{6,7},{7,8},{8,9},{9,10},{10,1... | collective-permute-start | bytes 49160 | tf_op jit(solution)/shard_map/ppermute | solution.py:78
  155.8 8.5 %collective-permute-start.16 = (f32[4,128,8]{2,0,1:T(4,128)S(1)}, f32[4,128,8]{2,0,1:T(4,128)S(1)}, u32[]{:S(2)}, u32[]{:S(2)}) collective-permute-start(f32[4,128,8]{2,0,1:T(4,128)S(1)} %collective-permute-done.15), channel_id=1, source_target_pairs={{0,1},{1,2},{2,3},{3,4},{4,5},{5,6},{6,7},{7,8},{8,9},{9,10},{10,1... | collective-permute-start | bytes 49160 | tf_op jit(solution)/shard_map/ppermute | solution.py:78
  164.3 8.5 %collective-permute-start.17 = (f32[4,128,8]{2,0,1:T(4,128)S(1)}, f32[4,128,8]{2,0,1:T(4,128)S(1)}, u32[]{:S(2)}, u32[]{:S(2)}) collective-permute-start(f32[4,128,8]{2,0,1:T(4,128)S(1)} %collective-permute-done.16), channel_id=1, source_target_pairs={{0,1},{1,2},{2,3},{3,4},{4,5},{5,6},{6,7},{7,8},{8,9},{9,10},{10,1... | collective-permute-start | bytes 49160 | tf_op jit(solution)/shard_map/ppermute | solution.py:78
  172.8 8.5 %collective-permute-start.18 = (f32[4,128,8]{2,0,1:T(4,128)S(1)}, f32[4,128,8]{2,0,1:T(4,128)S(1)}, u32[]{:S(2)}, u32[]{:S(2)}) collective-permute-start(f32[4,128,8]{2,0,1:T(4,128)S(1)} %collective-permute-done.17), channel_id=1, source_target_pairs={{0,1},{1,2},{2,3},{3,4},{4,5},{5,6},{6,7},{7,8},{8,9},{9,10},{10,1... | collective-permute-start | bytes 49160 | tf_op jit(solution)/shard_map/ppermute | solution.py:78
  181.3 0.7 copy-start.5
  182.0 8.6 %collective-permute-start.19 = (f32[4,128,8]{2,0,1:T(4,128)S(1)}, f32[4,128,8]{2,0,1:T(4,128)}, u32[]{:S(2)}, u32[]{:S(2)}) collective-permute-start(f32[4,128,8]{2,0,1:T(4,128)S(1)} %collective-permute-done.18), channel_id=1, source_target_pairs={{0,1},{1,2},{2,3},{3,4},{4,5},{5,6},{6,7},{7,8},{8,9},{9,10},{10,1... | collective-permute-start | bytes 49160 | tf_op jit(solution)/shard_map/ppermute | solution.py:78
  190.6 8.9 %collective-permute-start.20 = (f32[4,128,8]{2,0,1:T(4,128)}, f32[4,128,8]{2,0,1:T(4,128)}, u32[]{:S(2)}, u32[]{:S(2)}) collective-permute-start(f32[4,128,8]{2,0,1:T(4,128)} %collective-permute-done.19), channel_id=1, source_target_pairs={{0,1},{1,2},{2,3},{3,4},{4,5},{5,6},{6,7},{7,8},{8,9},{9,10},{10,1... | collective-permute-start | bytes 49160 | tf_op jit(solution)/shard_map/ppermute | solution.py:78
